TPU v7x, 32 devices: a whole 2x2x4 slice. The times are simulated.
32 devices in a mesh: groups: 2 (over y), seq: 8 (over z, core), panel: 2 (over x).
Axes of the slice: x: 2, y: 2, z: 4, core: 2. Of those that a mesh axis runs over, the one named last changes fastest.
Arguments:
- queries: bfloat16 [4096, 3072], P(('groups', 'seq'), 'panel'), parts along dimension 0, may hold values from -120 to 120
- key_rows: bfloat16 [4096, 3072], P(('groups', 'seq'), 'panel'), parts along dimension 0, may hold values from -6 to 6
- value_rows: bfloat16 [4096, 3072], P(('groups', 'seq'), 'panel'), parts along dimension 0, may hold values from -6 to 6
- block_lists: int32 [24, 16, 8], P('panel'), may hold values from 0 to 15, as said below
- block_counts: int32 [24, 16], P('panel'), may hold values from 4 to 8, as said below
Outputs:
- attended: bfloat16 [4096, 3072], P(('groups', 'seq', 'panel')), parts along dimension 0
There are 2 independent parts, one for each index of `groups`. A program takes and returns all parts, laid end to end along the dimension named above; an argument that names none is the same for every part. Nothing has to cross between parts.
Inputs may be any that keep to these rules, and one draw needn't show every extreme that they name: `block_lists`: entry 0 of each list is the tile's own block index; the entries of one list are distinct; for each head, the lists of the 2 tiles held by one index of seq name together at most 1 distinct blocks among the 2 blocks of any other index of seq, and exactly 1 of some other index. `block_counts`: some list has all 8 entries live.
All inputs are finite; a program needn't handle non-finite values.
Results may differ from a plain program's by a relative error of at most 0.008.
Values may be sent and summed in bfloat16 or wider, within the bound.
No kernel may reach another device: no remote copies, remote signals or barrier semaphores. Data moves between devices by JAX's collectives and lax.ppermute only.
A program may use at most 128 MiB of HBM per device.

v0:
```python
import functools

import jax
import jax.numpy as jnp
from jax import lax
from jax.experimental import pallas as pl
from jax.experimental.pallas import tpu as pltpu
from jax.sharding import PartitionSpec as P


HEAD_DIM = 128
BLOCK = 128
LOG2_E = 1.4426950408889634
DEAD = -1e30
CORES = 2
FIRST_SHARE = 7, 12
UNROLL = 7
VMEM_GRANT = 14 << 20
HOMES = 0, 4
STAGES = (
    ("early_0", ((0, 0, (0, 1), False), (0, 1, (0, 1), False)), ()),
    ("early_1", ((0, 0, (2, 3, 4, 5), True), (0, 1, (2, 3), True)), ()),
    (
        "early_2",
        ((1, 0, (0, 1, 2, 3, 4, 5), False),),
        (("chunk", 1, 1), ("chunk", 2, 1), ("chunk", 3, 1), ("query", 1, 0)),
    ),
    ("early_3", ((1, 1, (0, 1, 2, 3, 4, 5), False),), (("query", 1, 1),)),
    ("late_0", ((1, 0, (6, 7), True),), ()),
    ("late_3", ((0, 0, (6, 7), True),), ()),
    ("early_4", ((0, 1, (4, 5), True),), ()),
    ("late_1", ((1, 1, (6, 7), True),), ()),
    ("late_2", ((0, 1, (6, 7), True),), ()),
)


def tables(block_lists, block_counts, owner, seq_size):
    heads, tiles, listed = block_lists.shape
    per_index = tiles // seq_size
    lists = lax.dynamic_slice_in_dim(block_lists, owner * per_index, per_index, 1)
    counts = lax.dynamic_slice_in_dim(block_counts, owner * per_index, per_index, 1)
    slot_live = jnp.arange(listed, dtype=jnp.int32) < counts[:, :, None]
    ids = jnp.arange(tiles, dtype=jnp.int32)
    hits = (lists[:, :, :, None] == ids) & slot_live[:, :, :, None]
    keep = jnp.any(hits, axis=2).astype(jnp.int32).reshape(heads, per_index, seq_size, per_index)
    low, high = keep[..., 0], keep[..., 1]
    taken = jnp.max(high, axis=1)
    live = jnp.where(taken[:, None, :] == 1, high, low)
    other = jnp.where(taken[:, None, :] == 1, low, high)
    bits = jnp.array([2 << tile for tile in range(per_index)], jnp.int32)[None, :, None]
    code = taken + jnp.sum(live * bits, axis=1)
    code_other = (1 - taken) + jnp.sum(other * bits, axis=1)
    mine = jnp.arange(seq_size) == owner
    extra = jnp.sum(jnp.where(mine, code_other, 0), axis=1, keepdims=True)
    return jnp.concatenate([code, extra], axis=1)


def attend(query, codes, key_block, value_block):
    rows = query.shape[0]
    factor = HEAD_DIM ** (-0.5) * LOG2_E
    masked = []
    for j, code in enumerate(codes):
        scores = lax.dot_general(
            query, key_block(j, code & 1), (((1,), (1,)), ((), ())), preferred_element_type=jnp.float32
        )
        parts = []
        for tile in range(rows // BLOCK):
            bias = jnp.where((code >> (tile + 1)) & 1 == 1, 0.0, DEAD).astype(jnp.float32)
            parts.append(scores[tile * BLOCK : (tile + 1) * BLOCK] * factor + bias)
        masked.append(jnp.concatenate(parts, axis=0))
    top = jnp.max(functools.reduce(jnp.maximum, masked), axis=1, keepdims=True)
    total, mixed = None, None
    for j, code in enumerate(codes):
        weights = jnp.exp2(masked[j] - top)
        total = weights if total is None else total + weights
        product = jnp.dot(
            weights.astype(jnp.bfloat16), value_block(j, code & 1), preferred_element_type=jnp.float32
        )
        mixed = product if mixed is None else mixed + product
    return mixed / jnp.sum(total, axis=1, keepdims=True)


def gathered_kernel(seq_size, own_rows, info_ref, code_ref, query_ref, key_ref, value_ref, out_ref):
    head = pl.program_id(0)
    owner = info_ref[0]

    def block(ref):
        def read(j, which):
            index = owner if j == seq_size else j
            return ref[pl.ds(pl.multiple_of(index * own_rows + which * BLOCK, BLOCK), BLOCK), :]

        return read

    codes = [code_ref[head * (seq_size + 1) + j] for j in range(seq_size + 1)]
    out_ref[...] = attend(query_ref[...], codes, block(key_ref), block(value_ref)).astype(out_ref.dtype)


def gathered(queries, key_rows, value_rows, block_lists, block_counts, seq_size):
    rows, width = queries.shape
    heads = width // HEAD_DIM
    position = lax.axis_index("seq")
    keys = lax.all_gather(key_rows, "seq", axis=0, tiled=True)
    values = lax.all_gather(value_rows, "seq", axis=0, tiled=True)
    codes = tables(block_lists, block_counts, position, seq_size).reshape(-1)
    all_rows = keys.shape[0]
    out = pl.pallas_call(
        functools.partial(gathered_kernel, seq_size, rows),
        out_shape=jax.ShapeDtypeStruct((rows, width), queries.dtype),
        grid_spec=pltpu.PrefetchScalarGridSpec(
            num_scalar_prefetch=2,
            grid=(heads,),
            in_specs=[
                pl.BlockSpec((rows, HEAD_DIM), lambda h, *_: (0, h)),
                pl.BlockSpec((all_rows, HEAD_DIM), lambda h, *_: (0, h)),
                pl.BlockSpec((all_rows, HEAD_DIM), lambda h, *_: (0, h)),
            ],
            out_specs=pl.BlockSpec((rows, HEAD_DIM), lambda h, *_: (0, h)),
        ),
        name="attend_gathered",
    )(position.reshape(1), codes, queries, keys, values)
    return lax.all_to_all(out, "panel", split_axis=0, concat_axis=1, tiled=True)


def pieces_of(seq_pairs, panel_size, shift):
    return [
        (source * panel_size + panel, target * panel_size + (panel + shift) % panel_size)
        for source, target in seq_pairs
        for panel in range(panel_size)
    ]


def send(value, pairs, axes="seq"):
    return lax.ppermute(value, axes, pairs)


def pack_kernel(starts, sizes, chunk, *refs):
    sources, out, sems = refs[:-2], refs[-2], refs[-1]
    rows = sources[0].shape[0]
    columns = pl.ds(starts[chunk] * HEAD_DIM, sizes[chunk] * HEAD_DIM)
    copies = [
        pltpu.make_async_copy(ref.at[:, columns], out.at[pl.ds(kind * rows, rows), :], sems.at[kind])
        for kind, ref in enumerate(sources)
    ]
    for copy in copies:
        copy.start()
    for copy in copies:
        copy.wait()


def masked_scores(query, codes, key_block):
    factor = HEAD_DIM ** (-0.5) * LOG2_E
    masked = []
    for j, code in codes:
        scores = lax.dot_general(
            key_block(j, code & 1), query, (((1,), (1,)), ((), ())), preferred_element_type=jnp.float32
        )
        tiles = query.shape[0] // BLOCK
        bias = [
            jnp.full((1, BLOCK), jnp.where((code >> (tile + 1)) & 1 == 1, 0.0, DEAD), jnp.float32)
            for tile in range(tiles)
        ]
        masked.append(scores * factor + jnp.concatenate(bias, axis=1))
    return masked


def weigh(masked, top, codes, value_block):
    total, mixed = None, None
    for scores, (j, code) in zip(masked, codes):
        weights = jnp.exp2(scores - top)
        total = weights if total is None else total + weights
        product = lax.dot_general(
            value_block(j, code & 1),
            weights.astype(jnp.bfloat16),
            (((0,), (0,)), ((), ())),
            preferred_element_type=jnp.float32,
        )
        mixed = product if mixed is None else mixed + product
    return jnp.sum(total, axis=0, keepdims=True), mixed


def highest(masked):
    return jnp.max(functools.reduce(jnp.maximum, masked), axis=0, keepdims=True)


def each_unit(count, unit):
    groups = -(-count // UNROLL)
    size = -(-count // groups)
    whole = count // size

    @pl.loop(0, whole)
    def _(group):
        for i in range(size):
            unit(group * size, i)

    for i in range(count - whole * size):
        unit(whole * size, i)


def columns_of(head):
    return pl.ds(pl.multiple_of(head * HEAD_DIM, HEAD_DIM), HEAD_DIM)


def block_reader(pick):
    def block(slot, which):
        ref, first, columns = pick(slot)
        return ref[pl.ds(pl.multiple_of(first + which * BLOCK, BLOCK), BLOCK), columns]

    return block


def stage_kernel(seq_size, panel_size, heads, starts, sizes, jobs, keeps, inputs, final, *refs):
    info_ref, code_ref = refs[:2]
    have = dict(zip(inputs, refs[2:]))
    results = refs[2 + len(inputs) :]
    panel = info_ref[1]

    def job(n, side, k, slots, carry):
        queries = have["query", side, k]
        rows = queries.shape[0]
        piece = rows // panel_size

        def unit(base, i):
            h = base + i
            local = columns_of(h)
            first = (side * heads + h + starts[k]) * (seq_size + 1)
            codes = [(slot, code_ref[first + slot]) for slot in slots]
            if HOMES[side] in slots:
                codes.append((HOMES[side], code_ref[first + seq_size]))

            def pick(kind, slot):
                if ("chunk", slot, k) in have:
                    return have["chunk", slot, k], kind * rows, local
                return have["whole", slot, kind], 0, columns_of(h + starts[k])

            masked = masked_scores(queries[:, local], codes, block_reader(functools.partial(pick, 0)))
            top = highest(masked)
            if carry:
                stat = have["stat", side, k]
                before = stat[h, pl.ds(0, 1), :]
                top = jnp.maximum(before, top)
                kept = jnp.exp2(before - top)
            total, mixed = weigh(masked, top, codes, block_reader(functools.partial(pick, 1)))
            if carry:
                total = total + kept * stat[h, pl.ds(1, 1), :]
                mixed = mixed + kept * have["sum", side, k][h]
            if final:
                spare = results[-1]
                spare[i] = (mixed * (1.0 / total)).astype(spare.dtype).T
                for shift in range(panel_size):
                    first_row = pl.multiple_of(lax.rem(panel + shift, panel_size) * piece, piece)
                    results[n * panel_size + shift][:, local] = spare[i, pl.ds(first_row, piece), :]
            else:
                sums, stats = results[2 * n : 2 * n + 2]
                sums[h] = mixed
                stats[h, pl.ds(0, 1), :] = top
                stats[h, pl.ds(1, 1), :] = total

        each_unit(sizes[k], unit)

    @pl.when(info_ref[0] == 1)
    def _():
        for n, entry in enumerate(jobs):
            job(n, *entry)
        for n, (kind, which, k) in enumerate(keeps):
            copy = results[2 * len(jobs) + n]
            if kind == "query":
                copy[...] = have[kind, which, k][...]
                continue
            rows = copy.shape[0] // 2
            columns = pl.ds(starts[k] * HEAD_DIM, sizes[k] * HEAD_DIM)
            for half in range(2):
                copy[pl.ds(half * rows, rows), :] = have["whole", which, half][:, columns]


def assemble_kernel(panel_size, starts, sizes, aliased, info_ref, *refs):
    out_ref, sems = refs[-2:]
    refs = refs[1:] if aliased else refs
    count = len(sizes)
    width = out_ref.shape[1] // panel_size
    panel = info_ref[1]
    inner = info_ref[0] == 1
    copies = []
    for shift in range(panel_size):
        source = lax.rem(panel + panel_size - shift, panel_size)
        for chunk, (start, size) in enumerate(zip(starts, sizes)):
            columns = pl.ds(pl.multiple_of(source * width + start * HEAD_DIM, HEAD_DIM), size * HEAD_DIM)
            own, guest = (
                pltpu.make_async_copy(
                    refs[(side * count + chunk) * panel_size + shift],
                    out_ref.at[:, columns],
                    sems.at[shift, chunk],
                )
                for side in range(2)
            )
            pl.when(inner)(own.start)
            pl.when(jnp.logical_not(inner))(guest.start)
            copies.append(own)
    for copy in copies:
        copy.wait()


def relayed(queries, key_rows, value_rows, block_lists, block_counts, seq_size, panel_size):
    rows, width = queries.shape
    heads = width // HEAD_DIM
    chips = seq_size // CORES
    position = lax.axis_index("seq")
    panel = lax.axis_index("panel")
    chip, core = position // CORES, position % CORES
    last = chips - 1
    cores = range(CORES)
    inward = [(source * CORES + c, target * CORES + c) for source, target in ((0, 1), (last, last - 1)) for c in cores]
    across = [(source * CORES + c, target * CORES + c) for source, target in ((1, 2), (2, 1)) for c in cores]
    partner = [(z * CORES + c, z * CORES + CORES - 1 - c) for z in (1, 2) for c in cores]
    inner = [(z * CORES + c, z * CORES + c) for z in (1, 2) for c in cores]
    outward = [(target, source) for source, target in inward]
    in_vmem, in_smem, anywhere = (pl.BlockSpec(memory_space=s) for s in (pltpu.VMEM, pltpu.SMEM, pl.ANY))

    front = max(1, heads * FIRST_SHARE[0] // FIRST_SHARE[1])
    sizes = [front, heads - front]
    starts = [0, front]
    chunks = len(sizes)

    middle = [send(x, across) for x in (key_rows, value_rows)]

    def pack(chunk, *sources):
        return pl.pallas_call(
            functools.partial(pack_kernel, starts, sizes, chunk),
            out_shape=jax.ShapeDtypeStruct((len(sources) * rows, sizes[chunk] * HEAD_DIM), sources[0].dtype),
            in_specs=[anywhere] * len(sources),
            out_specs=in_vmem,
            scratch_shapes=[pltpu.SemaphoreType.DMA((len(sources),))],
            compiler_params=pltpu.CompilerParams(vmem_limit_bytes=VMEM_GRANT),
        )(*sources)

    packed = [pack(k, key_rows, value_rows) for k in range(chunks)]
    own_queries = [pack(k, queries) for k in range(chunks)]
    beside = [send(x, partner) for x in (key_rows, value_rows)]
    ends = [send(x, inward) for x in packed]
    guest_queries = [send(x, inward) for x in own_queries]
    middle_beside = [send(x, partner) for x in middle]

    is_inner = (chip >= 1) & (chip < last)
    end = jnp.where(chip * 2 < chips, 0, last)
    guest = end * CORES + core
    order = jnp.stack(
        [
            z * CORES + c
            for z in (chip, last - chip, end, last - end)
            for c in (core, CORES - 1 - core)
        ]
    )
    pick = (order[:, None] == jnp.arange(seq_size)).astype(jnp.int32)

    def arranged(owner):
        codes = tables(block_lists, block_counts, owner, seq_size)
        return jnp.concatenate([jnp.sum(codes[:, None, :seq_size] * pick, axis=2), codes[:, seq_size:]], axis=1)

    codes = jnp.stack([arranged(position), arranged(guest)]).reshape(-1)
    info = jnp.stack([is_inner.astype(jnp.int32), panel])

    ends_beside = [send(x, partner) for x in ends]
    far = [send(x, across) for x in ends]
    far_beside = [send(x, partner) for x in far]
    arrays = {}
    for slot, pair in ((1, beside), (2, middle), (3, middle_beside)):
        for kind in range(2):
            arrays["whole", slot, kind] = pair[kind]
    for k in range(chunks):
        arrays["query", 0, k], arrays["query", 1, k] = own_queries[k], guest_queries[k]
        for slot, parts in ((0, packed), (4, ends), (5, ends_beside), (6, far), (7, far_beside)):
            arrays["chunk", slot, k] = parts[k]

    pieces = {}
    both = ("seq", "panel")
    for name, jobs, keeps in STAGES:
        final = name.startswith("late")
        inputs = []
        for side, k, slots, carry in jobs:
            inputs.append(("query", side, k))
            for slot in slots:
                one = ("chunk", slot, k)
                inputs += [one] if one in arrays else [("whole", slot, kind) for kind in range(2)]
            if carry:
                inputs += [("sum", side, k), ("stat", side, k)]
        inputs = list(dict.fromkeys(inputs))
        if final:
            shapes = [
                jax.ShapeDtypeStruct((rows // panel_size, sizes[k] * HEAD_DIM), queries.dtype)
                for _, k, _, _ in jobs
                for _ in range(panel_size)
            ]
        else:
            shapes = [
                jax.ShapeDtypeStruct((sizes[k], height, rows), jnp.float32)
                for _, k, _, _ in jobs
                for height in (HEAD_DIM, 8)
            ]
            shapes += [
                jax.ShapeDtypeStruct(((1 if kind == "query" else 2) * rows, sizes[k] * HEAD_DIM), queries.dtype)
                for kind, _, k in keeps
            ]
        blocks = sum(sizes[k] * (len(slots) + (HOMES[side] in slots)) for side, k, slots, _ in jobs)
        results = pl.pallas_call(
            functools.partial(stage_kernel, seq_size, panel_size, heads, starts, sizes, jobs, keeps, inputs, final),
            out_shape=shapes,
            in_specs=[in_smem] * 2 + [in_vmem] * len(inputs),
            out_specs=[in_vmem] * len(shapes),
            scratch_shapes=[pltpu.VMEM((UNROLL, rows, HEAD_DIM), queries.dtype)] if final else [],
            compiler_params=pltpu.CompilerParams(vmem_limit_bytes=VMEM_GRANT),
            cost_estimate=pl.CostEstimate(
                flops=4 * rows * blocks * BLOCK * HEAD_DIM,
                bytes_accessed=blocks * 4 * BLOCK * HEAD_DIM,
                transcendentals=rows * blocks * BLOCK,
            ),
        )(info, codes, *(arrays[key] for key in inputs))
        if not final:
            for n, (side, k, _, _) in enumerate(jobs):
                arrays["sum", side, k], arrays["stat", side, k] = results[2 * n : 2 * n + 2]
            arrays.update(zip(keeps, results[2 * len(jobs) :]))
            continue
        for n, (side, k, _, _) in enumerate(jobs):
            for shift in range(panel_size):
                piece = results[n * panel_size + shift]
                if side == 1:
                    piece = send(piece, pieces_of(outward, panel_size, shift), both)
                elif shift:
                    piece = send(piece, pieces_of(inner, panel_size, shift), both)
                pieces[side, k, shift] = piece

    out = None
    for first, final in ((0, chunks - 1), (chunks - 1, chunks)):
        parts = [
            pieces[side, k, shift] for side in range(2) for k in range(first, final) for shift in range(panel_size)
        ]
        before = [] if out is None else [out]
        out = pl.pallas_call(
            functools.partial(assemble_kernel, panel_size, starts[first:final], sizes[first:final], len(before)),
            out_shape=jax.ShapeDtypeStruct((rows // panel_size, width * panel_size), queries.dtype),
            in_specs=[in_smem] + [anywhere] * len(before) + [in_vmem] * len(parts),
            out_specs=anywhere,
            scratch_shapes=[pltpu.SemaphoreType.DMA((panel_size, final - first))],
            input_output_aliases={1: 0} if before else {},
            compiler_params=pltpu.CompilerParams(vmem_limit_bytes=VMEM_GRANT),
        )(info, *before, *parts)
    return out


def solution(mesh):
    seq_size, panel_size = mesh.shape["seq"], mesh.shape["panel"]
    relay = seq_size // CORES - 2 == 2
    if relay:
        body = functools.partial(relayed, seq_size=seq_size, panel_size=panel_size)
    else:
        body = functools.partial(gathered, seq_size=seq_size)
    return jax.shard_map(
        body,
        mesh=mesh,
        in_specs=(
            P(("groups", "seq"), "panel"),
            P(("groups", "seq"), "panel"),
            P(("groups", "seq"), "panel"),
            P("panel", None, None),
            P("panel", None),
        ),
        out_specs=P(("groups", "seq", "panel"), None),
        check_vma=False,
    )
```

profile of v0, /device:TPU:0, one launch (start us, length us, event | category | flops | bytes accessed | tf_op | source)
XLA Modules:
  0.0 138.9 jit_solution(8675609795063267384)
XLA Ops:
  0.0 1.5 %collective-permute-start.3 = (bf16[256,1536]{1,0:T(8,128)(2,1)}, bf16[256,1536]{1,0:T(8,128)(2,1)}, u32[]{:S(2)}, u32[]{:S(2)}) collective-permute-start(bf16[256,1536]{1,0:T(8,128)(2,1)} %refs_0_.7), channel_id=1, source_target_pairs={{4,8},{6,10},{8,4},{10,6},{5,9},{7,11},{9,5},{11,7},{20,24},{22,26... | collective-permute-start | bytes 2359304 | tf_op jit(solution)/shard_map/ppermute | solution.py:133
  1.5 1.5 %collective-permute-start.4 = (bf16[256,1536]{1,0:T(8,128)(2,1)}, bf16[256,1536]{1,0:T(8,128)(2,1)}, u32[]{:S(2)}, u32[]{:S(2)}) collective-permute-start(bf16[256,1536]{1,0:T(8,128)(2,1)} %refs_1_.3), channel_id=1, source_target_pairs={{4,8},{6,10},{8,4},{10,6},{5,9},{7,11},{9,5},{11,7},{20,24},{22,26... | collective-permute-start | bytes 2359304 | tf_op jit(solution)/shard_map/ppermute | solution.py:133
  3.1 1.1 copy-done
  4.2 1.1 shard_map.74.refs_3_
  5.3 8.8 %collective-permute-start = (bf16[512,896]{1,0:T(8,128)(2,1)S(1)}, bf16[512,896]{1,0:T(8,128)(2,1)}, u32[]{:S(2)}, u32[]{:S(2)}) collective-permute-start(bf16[512,896]{1,0:T(8,128)(2,1)S(1)} %shard_map.74.refs_3_), channel_id=1, source_target_pairs={{0,4},{2,6},{12,8},{14,10},{1,5},{3,7},{13,9},{15,11},{16,20},{18,... | collective-permute-start | bytes 2752520 | tf_op jit(solution)/shard_map/ppermute | solution.py:133
  14.2 1.3 collective-permute-start.11
  15.5 1.0 shard_map.76.refs_7_.refs_3_
  16.6 2.3 %collective-permute-start.14 = (bf16[512,640]{1,0:T(8,128)(2,1)S(1)}, bf16[512,640]{1,0:T(8,128)(2,1)}, u32[]{:S(2)}, u32[]{:S(2)}) collective-permute-start(bf16[512,640]{1,0:T(8,128)(2,1)S(1)} %shard_map.76.refs_7_.refs_3_), channel_id=1, source_target_pairs={{0,4},{2,6},{12,8},{14,10},{1,5},{3,7},{13,9},{15,11},{16,20},{18,... | collective-permute-start | bytes 1966088 | tf_op jit(solution)/shard_map/ppermute | solution.py:133
  18.9 0.1 copy.22
  19.1 0.6 copy-done.7
  20.2 0.1 fusion.3
  20.5 23.3 %collective-permute-done.11.refs_2_ = bf16[256,896]{1,0:T(8,128)(2,1)S(1)} collective-permute-done((bf16[256,896]{1,0:T(8,128)(2,1)S(1)}, bf16[256,896]{1,0:T(8,128)(2,1)S(1)}, u32[]{:S(2)}, u32[]{:S(2)}) %collective-permute-start.11) | collective-permute-done | bytes 458784 | tf_op jit(solution)/shard_map/ppermute | solution.py:133
  43.8 0.8 copy-done.4
  44.6 1.6 %collective-permute-start.8 = (bf16[256,1536]{1,0:T(8,128)(2,1)}, bf16[256,1536]{1,0:T(8,128)(2,1)}, u32[]{:S(2)}, u32[]{:S(2)}) collective-permute-start(bf16[256,1536]{1,0:T(8,128)(2,1)} %refs_0_.7), channel_id=1, source_target_pairs={{4,6},{6,4},{8,10},{10,8},{5,7},{7,5},{9,11},{11,9},{20,22},{22,20... | collective-permute-start | bytes 2359304 | tf_op jit(solution)/shard_map/ppermute | solution.py:133
  46.1 0.7 collective-permute-start.1
  46.9 9.2 %collective-permute-done.14.refs_3_.refs_7_ = bf16[512,640]{1,0:T(8,128)(2,1)} collective-permute-done((bf16[512,640]{1,0:T(8,128)(2,1)S(1)}, bf16[512,640]{1,0:T(8,128)(2,1)}, u32[]{:S(2)}, u32[]{:S(2)}) %collective-permute-start.14) | collective-permute-done | bytes 655392 | tf_op jit(solution)/shard_map/ppermute | solution.py:133
  56.1 1.6 %collective-permute-start.9 = (bf16[256,1536]{1,0:T(8,128)(2,1)}, bf16[256,1536]{1,0:T(8,128)(2,1)}, u32[]{:S(2)}, u32[]{:S(2)}) collective-permute-start(bf16[256,1536]{1,0:T(8,128)(2,1)} %refs_1_.3), channel_id=1, source_target_pairs={{4,6},{6,4},{8,10},{10,8},{5,7},{7,5},{9,11},{11,9},{20,22},{22,20... | collective-permute-start | bytes 2359304 | tf_op jit(solution)/shard_map/ppermute | solution.py:133
  57.7 0.7 copy-done.8
  58.4 1.6 %collective-permute-start.5 = (bf16[256,1536]{1,0:T(8,128)(2,1)}, bf16[256,1536]{1,0:T(8,128)(2,1)}, u32[]{:S(2)}, u32[]{:S(2)}) collective-permute-start(bf16[256,1536]{1,0:T(8,128)(2,1)} %collective-permute-done.3.refs_3_.refs_6_), channel_id=1, source_target_pairs={{4,6},{6,4},{8,10},{10,8},{5,7},{7,5},{9,11},{11,9},{20,22},{22,20... | collective-permute-start | bytes 2359304 | tf_op jit(solution)/shard_map/ppermute | solution.py:133
  60.2 1.6 %collective-permute-start.15 = (bf16[512,640]{1,0:T(8,128)(2,1)}, bf16[512,640]{1,0:T(8,128)(2,1)}, u32[]{:S(2)}, u32[]{:S(2)}) collective-permute-start(bf16[512,640]{1,0:T(8,128)(2,1)} %collective-permute-done.14.refs_3_.refs_7_), channel_id=1, source_target_pairs={{4,8},{6,10},{8,4},{10,6},{5,9},{7,11},{9,5},{11,7},{20,24},{22,26... | collective-permute-start | bytes 1966088 | tf_op jit(solution)/shard_map/ppermute | solution.py:133
  61.7 1.6 %collective-permute-start.7 = (bf16[512,896]{1,0:T(8,128)(2,1)}, bf16[512,896]{1,0:T(8,128)(2,1)}, u32[]{:S(2)}, u32[]{:S(2)}) collective-permute-start(bf16[512,896]{1,0:T(8,128)(2,1)} %collective-permute-done.refs_7_.refs_10_), channel_id=1, source_target_pairs={{4,6},{6,4},{8,10},{10,8},{5,7},{7,5},{9,11},{11,9},{20,22},{22,20... | collective-permute-start | bytes 2752520 | tf_op jit(solution)/shard_map/ppermute | solution.py:133
  63.4 1.5 %collective-permute-start.6 = (bf16[256,1536]{1,0:T(8,128)(2,1)}, bf16[256,1536]{1,0:T(8,128)(2,1)}, u32[]{:S(2)}, u32[]{:S(2)}) collective-permute-start(bf16[256,1536]{1,0:T(8,128)(2,1)} %collective-permute-done.4.refs_4_.refs_7_), channel_id=1, source_target_pairs={{4,6},{6,4},{8,10},{10,8},{5,7},{7,5},{9,11},{11,9},{20,22},{22,20... | collective-permute-start | bytes 2359304 | tf_op jit(solution)/shard_map/ppermute | solution.py:133
  64.9 1.6 %collective-permute-start.2 = (bf16[512,896]{1,0:T(8,128)(2,1)S(1)}, bf16[512,896]{1,0:T(8,128)(2,1)}, u32[]{:S(2)}, u32[]{:S(2)}) collective-permute-start(bf16[512,896]{1,0:T(8,128)(2,1)S(1)} %collective-permute-done.1.refs_3_), channel_id=1, source_target_pairs={{4,6},{6,4},{8,10},{10,8},{5,7},{7,5},{9,11},{11,9},{20,22},{22,20... | collective-permute-start | bytes 2752520 | tf_op jit(solution)/shard_map/ppermute | solution.py:133
  66.8 1.5 %collective-permute-start.17 = (bf16[512,640]{1,0:T(8,128)(2,1)}, bf16[512,640]{1,0:T(8,128)(2,1)}, u32[]{:S(2)}, u32[]{:S(2)}) collective-permute-start(bf16[512,640]{1,0:T(8,128)(2,1)} %collective-permute-done.14.refs_3_.refs_7_), channel_id=1, source_target_pairs={{4,6},{6,4},{8,10},{10,8},{5,7},{7,5},{9,11},{11,9},{20,22},{22,20... | collective-permute-start | bytes 1966088 | tf_op jit(solution)/shard_map/ppermute | solution.py:133
  68.3 1.6 %collective-permute-start.16 = (bf16[512,640]{1,0:T(8,128)(2,1)}, bf16[512,640]{1,0:T(8,128)(2,1)}, u32[]{:S(2)}, u32[]{:S(2)}) collective-permute-start(bf16[512,640]{1,0:T(8,128)(2,1)} %collective-permute-done.15.refs_3_), channel_id=1, source_target_pairs={{4,6},{6,4},{8,10},{10,8},{5,7},{7,5},{9,11},{11,9},{20,22},{22,20... | collective-permute-start | bytes 1966088 | tf_op jit(solution)/shard_map/ppermute | solution.py:133
  69.9 1.1 copy-done.3
  71.4 24.4 %collective-permute-start.19 = (bf16[256,640]{1,0:T(8,128)(2,1)S(1)}, bf16[256,640]{1,0:T(8,128)(2,1)S(1)}, u32[]{:S(2)}, u32[]{:S(2)}) collective-permute-start(bf16[256,640]{1,0:T(8,128)(2,1)S(1)} %shard_map.75.refs_6_.refs_11_.refs_2_), channel_id=1, source_target_pairs={{0,4},{2,6},{12,8},{14,10},{1,5},{3,7},{13,9},{15,11},{16,20},{18,... | collective-permute-start | bytes 983048 | tf_op jit(solution)/shard_map/ppermute | solution.py:133
  95.9 1.0 copy-done.5
  96.9 2.9 %shard_map.80 = (f32[7,128,256]{2,1,0:T(8,128)S(1)}, f32[7,8,256]{2,1,0:T(8,128)S(1)}, bf16[512,640]{1,0:T(8,128)(2,1)S(1)}, bf16[512,640]{1,0:T(8,128)(2,1)S(1)...) custom-call(s32[2]{0:T(128)S(1)} %pad_add_fusion.3.refs_0_.info_ref, s32[216]{0:T(256)S(1)} %reshape.60.refs_1_, ...), custom_call_target="tpu_custom_call" | custom-call | flops 822083584 | bytes 3211264 | tf_op jit(solution)/shard_map/pallas_call | solution.py:403
  99.8 1.2 shard_map.81
  101.0 1.3 collective-permute-start.12
  102.3 1.4 %shard_map.77 = (f32[7,128,256]{2,1,0:T(8,128)S(1)}, f32[7,8,256]{2,1,0:T(8,128)S(1)}, f32[5,128,256]{2,1,0:T(8,128)S(1)}, f32[5,8,256]{2,1,0:T(8,128)S(1)}) custom-call(s32[2]{0:T(128)S(1)} %pad_add_fusion.3.refs_0_.info_ref, s32[216]{0:T(256)S(1)} %reshape.60.refs_1_, bf16[256,896]{1,0:T(8,128)(2,1)S(1)} %shard_map.73.refs_2_, ...), custom_call_target="tpu_custom_call" | custom-call | flops 603979776 | bytes 2359296 | tf_op jit(solution)/shard_map/pallas_call | solution.py:403
  103.7 2.4 %shard_map.78 = (f32[7,128,256]{2,1,0:T(8,128)S(1)}, f32[7,8,256]{2,1,0:T(8,128)S(1)}, f32[5,128,256]{2,1,0:T(8,128)S(1)}, f32[5,8,256]{2,1,0:T(8,128)S(1)}) custom-call(s32[2]{0:T(128)S(1)} %pad_add_fusion.3.refs_0_.info_ref, s32[216]{0:T(256)S(1)} %reshape.60.refs_1_, bf16[256,896]{1,0:T(8,128)(2,1)S(1)} %shard_map.73.refs_2_, ...), custom_call_target="tpu_custom_call" | custom-call | flops 637534208 | bytes 2490368 | tf_op jit(solution)/shard_map/pallas_call | solution.py:403
  106.1 1.3 collective-permute-start.13
  107.4 1.2 shard_map.79
  108.7 0.7 collective-permute-start.10
  109.3 1.5 %shard_map.85 = (f32[5,128,256]{2,1,0:T(8,128)S(1)}, f32[5,8,256]{2,1,0:T(8,128)S(1)}, bf16[256,640]{1,0:T(8,128)(2,1)S(1)}) custom-call(s32[2]{0:T(128)S(1)} %pad_add_fusion.3.refs_0_.info_ref, s32[216]{0:T(256)S(1)} %reshape.60.refs_1_, bf16[256,640]{1,0:T(8,128)(2,1)S(1)} %collective-permute-done.19.refs_2_, ...), custom_call_target="tpu_custom_call" | custom-call | flops 587202560 | bytes 2293760 | tf_op jit(solution)/shard_map/pallas_call | solution.py:403
  110.8 1.3 shard_map.83
  112.2 1.3 shard_map.86
  113.5 1.3 collective-permute-start.20
  114.8 1.3 collective-permute-start.21
  116.1 1.3 shard_map.84
  117.4 0.7 collective-permute-start.18
  118.1 3.4 %collective-permute-done.13.refs_3_ = bf16[128,896]{1,0:T(8,128)(2,1)S(1)} collective-permute-done((bf16[128,896]{1,0:T(8,128)(2,1)S(1)}, bf16[128,896]{1,0:T(8,128)(2,1)S(1)}, u32[]{:S(2)}, u32[]{:S(2)}) %collective-permute-start.13) | collective-permute-done | bytes 229408 | tf_op jit(solution)/shard_map/ppermute | solution.py:133
  121.5 1.3 shard_map.82.refs_0_
  122.8 12.1 %collective-permute-done.20.refs_3_ = bf16[128,640]{1,0:T(8,128)(2,1)S(1)} collective-permute-done((bf16[128,640]{1,0:T(8,128)(2,1)S(1)}, bf16[128,640]{1,0:T(8,128)(2,1)S(1)}, u32[]{:S(2)}, u32[]{:S(2)}) %collective-permute-start.20) | collective-permute-done | bytes 163872 | tf_op jit(solution)/shard_map/ppermute | solution.py:133
  134.9 2.5 %collective-permute-done.21.refs_4_ = bf16[128,640]{1,0:T(8,128)(2,1)S(1)} collective-permute-done((bf16[128,640]{1,0:T(8,128)(2,1)S(1)}, bf16[128,640]{1,0:T(8,128)(2,1)S(1)}, u32[]{:S(2)}, u32[]{:S(2)}) %collective-permute-start.21) | collective-permute-done | bytes 163872 | tf_op jit(solution)/shard_map/ppermute | solution.py:133
  137.5 1.3 shard_map.87
  (60 shorter events, 1.8 us)
Async XLA Ops:
  0.0 58.4 %collective-permute-start.3 = (bf16[256,1536]{1,0:T(8,128)(2,1)}, bf16[256,1536]{1,0:T(8,128)(2,1)}, u32[]{:S(2)}, u32[]{:S(2)}) collective-permute-start(bf16[256,1536]{1,0:T(8,128)(2,1)} %refs_0_.7), channel_id=1, source_target_pairs={{4,8},{6,10},{8,4},{10,6},{5,9},{7,11},{9,5},{11,7},{20,24},{22,26... | collective-permute-start | bytes 2359304 | tf_op jit(solution)/shard_map/ppermute | solution.py:133
  1.5 58.6 %collective-permute-start.4 = (bf16[256,1536]{1,0:T(8,128)(2,1)}, bf16[256,1536]{1,0:T(8,128)(2,1)}, u32[]{:S(2)}, u32[]{:S(2)}) collective-permute-start(bf16[256,1536]{1,0:T(8,128)(2,1)} %refs_1_.3), channel_id=1, source_target_pairs={{4,8},{6,10},{8,4},{10,6},{5,9},{7,11},{9,5},{11,7},{20,24},{22,26... | collective-permute-start | bytes 2359304 | tf_op jit(solution)/shard_map/ppermute | solution.py:133
  3.1 1.1 copy-start
  4.2 9.9 %copy-start.2 = (bf16[256,1536]{1,0:T(8,128)(2,1)S(1)}, bf16[256,1536]{1,0:T(8,128)(2,1)}, u32[]{:S(2)}) copy-start(bf16[256,1536]{1,0:T(8,128)(2,1)} %refs_0_.6) | copy-start | bytes 2359300
  5.3 10.2 %copy-start.1 = (bf16[256,1536]{1,0:T(8,128)(2,1)S(1)}, bf16[256,1536]{1,0:T(8,128)(2,1)}, u32[]{:S(2)}) copy-start(bf16[256,1536]{1,0:T(8,128)(2,1)} %refs_1_.3) | copy-start | bytes 2359300
  5.3 40.8 %collective-permute-start = (bf16[512,896]{1,0:T(8,128)(2,1)S(1)}, bf16[512,896]{1,0:T(8,128)(2,1)}, u32[]{:S(2)}, u32[]{:S(2)}) collective-permute-start(bf16[512,896]{1,0:T(8,128)(2,1)S(1)} %shard_map.74.refs_3_), channel_id=1, source_target_pairs={{0,4},{2,6},{12,8},{14,10},{1,5},{3,7},{13,9},{15,11},{16,20},{18,... | collective-permute-start | bytes 2752520 | tf_op jit(solution)/shard_map/ppermute | solution.py:133
  14.2 29.6 %collective-permute-start.11 = (bf16[256,896]{1,0:T(8,128)(2,1)S(1)}, bf16[256,896]{1,0:T(8,128)(2,1)S(1)}, u32[]{:S(2)}, u32[]{:S(2)}) collective-permute-start(bf16[256,896]{1,0:T(8,128)(2,1)S(1)} %shard_map.73.refs_2_), channel_id=1, source_target_pairs={{0,4},{2,6},{12,8},{14,10},{1,5},{3,7},{13,9},{15,11},{16,20},{18,... | collective-permute-start | bytes 1376264 | tf_op jit(solution)/shard_map/ppermute | solution.py:133
  16.5 2.3 %copy-start.6 = (s32[12,16,8]{1,2,0:T(8,128)S(1)}, s32[12,16,8]{1,2,0:T(8,128)}, u32[]{:S(2)}) copy-start(s32[12,16,8]{1,2,0:T(8,128)} %param.10) | copy-start | bytes 18436
  16.6 39.6 %collective-permute-start.14 = (bf16[512,640]{1,0:T(8,128)(2,1)S(1)}, bf16[512,640]{1,0:T(8,128)(2,1)}, u32[]{:S(2)}, u32[]{:S(2)}) collective-permute-start(bf16[512,640]{1,0:T(8,128)(2,1)S(1)} %shard_map.76.refs_7_.refs_3_), channel_id=1, source_target_pairs={{0,4},{2,6},{12,8},{14,10},{1,5},{3,7},{13,9},{15,11},{16,20},{18,... | collective-permute-start | bytes 1966088 | tf_op jit(solution)/shard_map/ppermute | solution.py:133
  18.9 0.7 copy-start.7
  43.8 0.8 copy-start.4
  44.6 17.2 %collective-permute-start.8 = (bf16[256,1536]{1,0:T(8,128)(2,1)}, bf16[256,1536]{1,0:T(8,128)(2,1)}, u32[]{:S(2)}, u32[]{:S(2)}) collective-permute-start(bf16[256,1536]{1,0:T(8,128)(2,1)} %refs_0_.7), channel_id=1, source_target_pairs={{4,6},{6,4},{8,10},{10,8},{5,7},{7,5},{9,11},{11,9},{20,22},{22,20... | collective-permute-start | bytes 2359304 | tf_op jit(solution)/shard_map/ppermute | solution.py:133
  46.1 18.8 %collective-permute-start.1 = (bf16[512,896]{1,0:T(8,128)(2,1)}, bf16[512,896]{1,0:T(8,128)(2,1)S(1)}, u32[]{:S(2)}, u32[]{:S(2)}) collective-permute-start(bf16[512,896]{1,0:T(8,128)(2,1)} %collective-permute-done.refs_7_.refs_10_), channel_id=1, source_target_pairs={{4,8},{6,10},{8,4},{10,6},{5,9},{7,11},{9,5},{11,7},{20,24},{22,26... | collective-permute-start | bytes 2752520 | tf_op jit(solution)/shard_map/ppermute | solution.py:133
  56.1 7.3 %collective-permute-start.9 = (bf16[256,1536]{1,0:T(8,128)(2,1)}, bf16[256,1536]{1,0:T(8,128)(2,1)}, u32[]{:S(2)}, u32[]{:S(2)}) collective-permute-start(bf16[256,1536]{1,0:T(8,128)(2,1)} %refs_1_.3), channel_id=1, source_target_pairs={{4,6},{6,4},{8,10},{10,8},{5,7},{7,5},{9,11},{11,9},{20,22},{22,20... | collective-permute-start | bytes 2359304 | tf_op jit(solution)/shard_map/ppermute | solution.py:133
  57.7 0.7 copy-start.8
  58.4 9.9 %collective-permute-start.5 = (bf16[256,1536]{1,0:T(8,128)(2,1)}, bf16[256,1536]{1,0:T(8,128)(2,1)}, u32[]{:S(2)}, u32[]{:S(2)}) collective-permute-start(bf16[256,1536]{1,0:T(8,128)(2,1)} %collective-permute-done.3.refs_3_.refs_6_), channel_id=1, source_target_pairs={{4,6},{6,4},{8,10},{10,8},{5,7},{7,5},{9,11},{11,9},{20,22},{22,20... | collective-permute-start | bytes 2359304 | tf_op jit(solution)/shard_map/ppermute | solution.py:133
  60.2 6.6 %collective-permute-start.15 = (bf16[512,640]{1,0:T(8,128)(2,1)}, bf16[512,640]{1,0:T(8,128)(2,1)}, u32[]{:S(2)}, u32[]{:S(2)}) collective-permute-start(bf16[512,640]{1,0:T(8,128)(2,1)} %collective-permute-done.14.refs_3_.refs_7_), channel_id=1, source_target_pairs={{4,8},{6,10},{8,4},{10,6},{5,9},{7,11},{9,5},{11,7},{20,24},{22,26... | collective-permute-start | bytes 1966088 | tf_op jit(solution)/shard_map/ppermute | solution.py:133
  61.7 34.1 %collective-permute-start.7 = (bf16[512,896]{1,0:T(8,128)(2,1)}, bf16[512,896]{1,0:T(8,128)(2,1)}, u32[]{:S(2)}, u32[]{:S(2)}) collective-permute-start(bf16[512,896]{1,0:T(8,128)(2,1)} %collective-permute-done.refs_7_.refs_10_), channel_id=1, source_target_pairs={{4,6},{6,4},{8,10},{10,8},{5,7},{7,5},{9,11},{11,9},{20,22},{22,20... | collective-permute-start | bytes 2752520 | tf_op jit(solution)/shard_map/ppermute | solution.py:133
  63.4 8.0 %collective-permute-start.6 = (bf16[256,1536]{1,0:T(8,128)(2,1)}, bf16[256,1536]{1,0:T(8,128)(2,1)}, u32[]{:S(2)}, u32[]{:S(2)}) collective-permute-start(bf16[256,1536]{1,0:T(8,128)(2,1)} %collective-permute-done.4.refs_4_.refs_7_), channel_id=1, source_target_pairs={{4,6},{6,4},{8,10},{10,8},{5,7},{7,5},{9,11},{11,9},{20,22},{22,20... | collective-permute-start | bytes 2359304 | tf_op jit(solution)/shard_map/ppermute | solution.py:133
  64.9 34.8 %collective-permute-start.2 = (bf16[512,896]{1,0:T(8,128)(2,1)S(1)}, bf16[512,896]{1,0:T(8,128)(2,1)}, u32[]{:S(2)}, u32[]{:S(2)}) collective-permute-start(bf16[512,896]{1,0:T(8,128)(2,1)S(1)} %collective-permute-done.1.refs_3_), channel_id=1, source_target_pairs={{4,6},{6,4},{8,10},{10,8},{5,7},{7,5},{9,11},{11,9},{20,22},{22,20... | collective-permute-start | bytes 2752520 | tf_op jit(solution)/shard_map/ppermute | solution.py:133
  66.8 42.6 %collective-permute-start.17 = (bf16[512,640]{1,0:T(8,128)(2,1)}, bf16[512,640]{1,0:T(8,128)(2,1)}, u32[]{:S(2)}, u32[]{:S(2)}) collective-permute-start(bf16[512,640]{1,0:T(8,128)(2,1)} %collective-permute-done.14.refs_3_.refs_7_), channel_id=1, source_target_pairs={{4,6},{6,4},{8,10},{10,8},{5,7},{7,5},{9,11},{11,9},{20,22},{22,20... | collective-permute-start | bytes 1966088 | tf_op jit(solution)/shard_map/ppermute | solution.py:133
  68.3 43.9 %collective-permute-start.16 = (bf16[512,640]{1,0:T(8,128)(2,1)}, bf16[512,640]{1,0:T(8,128)(2,1)}, u32[]{:S(2)}, u32[]{:S(2)}) collective-permute-start(bf16[512,640]{1,0:T(8,128)(2,1)} %collective-permute-done.15.refs_3_), channel_id=1, source_target_pairs={{4,6},{6,4},{8,10},{10,8},{5,7},{7,5},{9,11},{11,9},{20,22},{22,20... | collective-permute-start | bytes 1966088 | tf_op jit(solution)/shard_map/ppermute | solution.py:133
  69.9 1.1 copy-start.3
  71.4 37.3 %collective-permute-start.19 = (bf16[256,640]{1,0:T(8,128)(2,1)S(1)}, bf16[256,640]{1,0:T(8,128)(2,1)S(1)}, u32[]{:S(2)}, u32[]{:S(2)}) collective-permute-start(bf16[256,640]{1,0:T(8,128)(2,1)S(1)} %shard_map.75.refs_6_.refs_11_.refs_2_), channel_id=1, source_target_pairs={{0,4},{2,6},{12,8},{14,10},{1,5},{3,7},{13,9},{15,11},{16,20},{18,... | collective-permute-start | bytes 983048 | tf_op jit(solution)/shard_map/ppermute | solution.py:133
  95.9 1.0 copy-start.5
  101.0 16.4 %collective-permute-start.12 = (bf16[128,896]{1,0:T(8,128)(2,1)S(1)}, bf16[128,896]{1,0:T(8,128)(2,1)S(1)}, u32[]{:S(2)}, u32[]{:S(2)}) collective-permute-start(bf16[128,896]{1,0:T(8,128)(2,1)S(1)} %get-tuple-element.43), channel_id=1, source_target_pairs={{4,0},{5,1},{6,2},{7,3},{8,12},{9,13},{10,14},{11,15},{20,16},{21,... | collective-permute-start | bytes 688136 | tf_op jit(solution)/shard_map/ppermute | solution.py:133
  106.1 15.4 %collective-permute-start.13 = (bf16[128,896]{1,0:T(8,128)(2,1)S(1)}, bf16[128,896]{1,0:T(8,128)(2,1)S(1)}, u32[]{:S(2)}, u32[]{:S(2)}) collective-permute-start(bf16[128,896]{1,0:T(8,128)(2,1)S(1)} %get-tuple-element.44), channel_id=1, source_target_pairs={{4,1},{5,0},{6,3},{7,2},{8,13},{9,12},{10,15},{11,14},{20,17},{21,... | collective-permute-start | bytes 688136 | tf_op jit(solution)/shard_map/ppermute | solution.py:133
  108.7 12.8 %collective-permute-start.10 = (bf16[128,896]{1,0:T(8,128)(2,1)S(1)}, bf16[128,896]{1,0:T(8,128)(2,1)S(1)}, u32[]{:S(2)}, u32[]{:S(2)}) collective-permute-start(bf16[128,896]{1,0:T(8,128)(2,1)S(1)} %get-tuple-element.39), channel_id=1, source_target_pairs={{4,5},{5,4},{6,7},{7,6},{8,9},{9,8},{10,11},{11,10},{20,21},{21,20... | collective-permute-start | bytes 688136 | tf_op jit(solution)/shard_map/ppermute | solution.py:133
  113.5 21.4 %collective-permute-start.20 = (bf16[128,640]{1,0:T(8,128)(2,1)S(1)}, bf16[128,640]{1,0:T(8,128)(2,1)S(1)}, u32[]{:S(2)}, u32[]{:S(2)}) collective-permute-start(bf16[128,640]{1,0:T(8,128)(2,1)S(1)} %get-tuple-element.57), channel_id=1, source_target_pairs={{4,0},{5,1},{6,2},{7,3},{8,12},{9,13},{10,14},{11,15},{20,16},{21,... | collective-permute-start | bytes 491528 | tf_op jit(solution)/shard_map/ppermute | solution.py:133
  114.8 22.7 %collective-permute-start.21 = (bf16[128,640]{1,0:T(8,128)(2,1)S(1)}, bf16[128,640]{1,0:T(8,128)(2,1)S(1)}, u32[]{:S(2)}, u32[]{:S(2)}) collective-permute-start(bf16[128,640]{1,0:T(8,128)(2,1)S(1)} %get-tuple-element.58), channel_id=1, source_target_pairs={{4,1},{5,0},{6,3},{7,2},{8,13},{9,12},{10,15},{11,14},{20,17},{21,... | collective-permute-start | bytes 491528 | tf_op jit(solution)/shard_map/ppermute | solution.py:133
  117.4 20.1 %collective-permute-start.18 = (bf16[128,640]{1,0:T(8,128)(2,1)S(1)}, bf16[128,640]{1,0:T(8,128)(2,1)S(1)}, u32[]{:S(2)}, u32[]{:S(2)}) collective-permute-start(bf16[128,640]{1,0:T(8,128)(2,1)S(1)} %get-tuple-element.50), channel_id=1, source_target_pairs={{4,5},{5,4},{6,7},{7,6},{8,9},{9,8},{10,11},{11,10},{20,21},{21,20... | collective-permute-start | bytes 491528 | tf_op jit(solution)/shard_map/ppermute | solution.py:133
where the time goes:
time: 141 us; the launch traced here: 139 us
  starting transfers between devices  61.2 us (43%)
  waiting for transfers between devices  50.6 us (36%)
  Pallas kernels  19.3 us (14%)
  local copies, waits for them, and re-layouts  6.27 us (4%)
    ppermute x22, starting transfers between devices, send(): return lax.ppermute(value, axes, pairs)  61.2 us
    ppermute x22, waiting for transfers between devices, send(): return lax.ppermute(value, axes, pairs)  50.6 us
    pallas_call x9, Pallas kernels, relayed(): pl.pallas_call(functools.partial(stage_kernel, seq_size, panel_size, head...  14.5 us
    unnamed x18, local copies, waits for them, and re-layouts  5.28 us
  transfers between devices with their start and end apart: 22, of which 5 were waited for; matrix products, arithmetic and copies ran while one was open for 1% of the time, Pallas kernels for 13%

commit v1 on v0

--- a/solution.py
+++ b/solution.py
@@ -14,7 +14,7 @@
 DEAD = -1e30
 CORES = 2
 FIRST_SHARE = 7, 12
-UNROLL = 7
+UNROLL = 5
 VMEM_GRANT = 14 << 20
 HOMES = 0, 4
 STAGES = (
@@ -25,10 +25,9 @@
         ((1, 0, (0, 1, 2, 3, 4, 5), False),),
         (("chunk", 1, 1), ("chunk", 2, 1), ("chunk", 3, 1), ("query", 1, 0)),
     ),
-    ("early_3", ((1, 1, (0, 1, 2, 3, 4, 5), False),), (("query", 1, 1),)),
+    ("early_3", ((1, 1, (0, 1, 2, 3, 4, 5), False), (0, 1, (4, 5), True)), (("query", 1, 1),)),
     ("late_0", ((1, 0, (6, 7), True),), ()),
     ("late_3", ((0, 0, (6, 7), True),), ()),
-    ("early_4", ((0, 1, (4, 5), True),), ()),
     ("late_1", ((1, 1, (6, 7), True),), ()),
     ("late_2", ((0, 1, (6, 7), True),), ()),
 )

time: 141 us -> 139 us (0.986)
    pallas_call x9 -> x8, Pallas kernels: 14.5 us -> 13.2 us  [relayed(): pl.pallas_call(functools.partial(stage_kernel, seq_size, panel_size, head...]
  transfers between devices with their start and end apart: 22 -> 22, of which waited for: 5 -> 5; matrix products, arithmetic and copies ran while one was open for 1% -> 1% of each run, Pallas kernels for 13% -> 12%
where the time goes in v1:
time: 139 us; the launch traced here: 137 us
  starting transfers between devices  61.2 us (44%)
  waiting for transfers between devices  50.2 us (36%)
  Pallas kernels  18 us (13%)
  local copies, waits for them, and re-layouts  6.27 us (5%)
    ppermute x22, starting transfers between devices, send(): return lax.ppermute(value, axes, pairs)  61.2 us
    ppermute x22, waiting for transfers between devices, send(): return lax.ppermute(value, axes, pairs)  50.2 us
    pallas_call x8, Pallas kernels, relayed(): pl.pallas_call(functools.partial(stage_kernel, seq_size, panel_size, head...  13.2 us
    unnamed x18, local copies, waits for them, and re-layouts  5.28 us
  transfers between devices with their start and end apart: 22, of which 5 were waited for; matrix products, arithmetic and copies ran while one was open for 1% of the time, Pallas kernels for 12%

profile of v1, /device:TPU:0, one launch (start us, length us, event | category | flops | bytes accessed | tf_op | source)
XLA Modules:
  0.0 137.2 jit_solution(8318703138987075196)
XLA Ops:
  0.0 1.5 %collective-permute-start.3 = (bf16[256,1536]{1,0:T(8,128)(2,1)}, bf16[256,1536]{1,0:T(8,128)(2,1)}, u32[]{:S(2)}, u32[]{:S(2)}) collective-permute-start(bf16[256,1536]{1,0:T(8,128)(2,1)} %refs_0_.7), channel_id=1, source_target_pairs={{4,8},{6,10},{8,4},{10,6},{5,9},{7,11},{9,5},{11,7},{20,24},{22,26... | collective-permute-start | bytes 2359304 | tf_op jit(solution)/shard_map/ppermute | solution.py:132
  1.5 1.5 %collective-permute-start.4 = (bf16[256,1536]{1,0:T(8,128)(2,1)}, bf16[256,1536]{1,0:T(8,128)(2,1)}, u32[]{:S(2)}, u32[]{:S(2)}) collective-permute-start(bf16[256,1536]{1,0:T(8,128)(2,1)} %refs_1_.3), channel_id=1, source_target_pairs={{4,8},{6,10},{8,4},{10,6},{5,9},{7,11},{9,5},{11,7},{20,24},{22,26... | collective-permute-start | bytes 2359304 | tf_op jit(solution)/shard_map/ppermute | solution.py:132
  3.1 1.1 copy-done
  4.2 1.1 shard_map.74.refs_3_
  5.3 8.8 %collective-permute-start = (bf16[512,896]{1,0:T(8,128)(2,1)S(1)}, bf16[512,896]{1,0:T(8,128)(2,1)}, u32[]{:S(2)}, u32[]{:S(2)}) collective-permute-start(bf16[512,896]{1,0:T(8,128)(2,1)S(1)} %shard_map.74.refs_3_), channel_id=1, source_target_pairs={{0,4},{2,6},{12,8},{14,10},{1,5},{3,7},{13,9},{15,11},{16,20},{18,... | collective-permute-start | bytes 2752520 | tf_op jit(solution)/shard_map/ppermute | solution.py:132
  14.2 1.3 collective-permute-start.11
  15.5 1.0 shard_map.76.refs_7_.refs_3_
  16.6 2.3 %collective-permute-start.14 = (bf16[512,640]{1,0:T(8,128)(2,1)S(1)}, bf16[512,640]{1,0:T(8,128)(2,1)}, u32[]{:S(2)}, u32[]{:S(2)}) collective-permute-start(bf16[512,640]{1,0:T(8,128)(2,1)S(1)} %shard_map.76.refs_7_.refs_3_), channel_id=1, source_target_pairs={{0,4},{2,6},{12,8},{14,10},{1,5},{3,7},{13,9},{15,11},{16,20},{18,... | collective-permute-start | bytes 1966088 | tf_op jit(solution)/shard_map/ppermute | solution.py:132
  19.0 0.1 copy.22
  19.1 0.6 copy-done.7
  20.1 0.1 copy.25
  20.3 0.1 fusion.3
  20.5 23.3 %collective-permute-done.11.refs_2_ = bf16[256,896]{1,0:T(8,128)(2,1)S(1)} collective-permute-done((bf16[256,896]{1,0:T(8,128)(2,1)S(1)}, bf16[256,896]{1,0:T(8,128)(2,1)S(1)}, u32[]{:S(2)}, u32[]{:S(2)}) %collective-permute-start.11) | collective-permute-done | bytes 458784 | tf_op jit(solution)/shard_map/ppermute | solution.py:132
  43.8 0.8 copy-done.4
  44.6 1.6 %collective-permute-start.8 = (bf16[256,1536]{1,0:T(8,128)(2,1)}, bf16[256,1536]{1,0:T(8,128)(2,1)}, u32[]{:S(2)}, u32[]{:S(2)}) collective-permute-start(bf16[256,1536]{1,0:T(8,128)(2,1)} %refs_0_.7), channel_id=1, source_target_pairs={{4,6},{6,4},{8,10},{10,8},{5,7},{7,5},{9,11},{11,9},{20,22},{22,20... | collective-permute-start | bytes 2359304 | tf_op jit(solution)/shard_map/ppermute | solution.py:132
  46.1 0.7 collective-permute-start.1
  46.9 9.2 %collective-permute-done.14.refs_7_ = bf16[512,640]{1,0:T(8,128)(2,1)} collective-permute-done((bf16[512,640]{1,0:T(8,128)(2,1)S(1)}, bf16[512,640]{1,0:T(8,128)(2,1)}, u32[]{:S(2)}, u32[]{:S(2)}) %collective-permute-start.14) | collective-permute-done | bytes 655392 | tf_op jit(solution)/shard_map/ppermute | solution.py:132
  56.1 1.6 %collective-permute-start.9 = (bf16[256,1536]{1,0:T(8,128)(2,1)}, bf16[256,1536]{1,0:T(8,128)(2,1)}, u32[]{:S(2)}, u32[]{:S(2)}) collective-permute-start(bf16[256,1536]{1,0:T(8,128)(2,1)} %refs_1_.3), channel_id=1, source_target_pairs={{4,6},{6,4},{8,10},{10,8},{5,7},{7,5},{9,11},{11,9},{20,22},{22,20... | collective-permute-start | bytes 2359304 | tf_op jit(solution)/shard_map/ppermute | solution.py:132
  57.7 0.7 copy-done.8
  58.4 1.6 %collective-permute-start.5 = (bf16[256,1536]{1,0:T(8,128)(2,1)}, bf16[256,1536]{1,0:T(8,128)(2,1)}, u32[]{:S(2)}, u32[]{:S(2)}) collective-permute-start(bf16[256,1536]{1,0:T(8,128)(2,1)} %collective-permute-done.3.refs_3_.refs_6_), channel_id=1, source_target_pairs={{4,6},{6,4},{8,10},{10,8},{5,7},{7,5},{9,11},{11,9},{20,22},{22,20... | collective-permute-start | bytes 2359304 | tf_op jit(solution)/shard_map/ppermute | solution.py:132
  60.2 1.6 %collective-permute-start.15 = (bf16[512,640]{1,0:T(8,128)(2,1)}, bf16[512,640]{1,0:T(8,128)(2,1)}, u32[]{:S(2)}, u32[]{:S(2)}) collective-permute-start(bf16[512,640]{1,0:T(8,128)(2,1)} %collective-permute-done.14.refs_7_), channel_id=1, source_target_pairs={{4,8},{6,10},{8,4},{10,6},{5,9},{7,11},{9,5},{11,7},{20,24},{22,26... | collective-permute-start | bytes 1966088 | tf_op jit(solution)/shard_map/ppermute | solution.py:132
  61.7 1.6 %collective-permute-start.7 = (bf16[512,896]{1,0:T(8,128)(2,1)}, bf16[512,896]{1,0:T(8,128)(2,1)}, u32[]{:S(2)}, u32[]{:S(2)}) collective-permute-start(bf16[512,896]{1,0:T(8,128)(2,1)} %collective-permute-done.refs_7_.refs_10_), channel_id=1, source_target_pairs={{4,6},{6,4},{8,10},{10,8},{5,7},{7,5},{9,11},{11,9},{20,22},{22,20... | collective-permute-start | bytes 2752520 | tf_op jit(solution)/shard_map/ppermute | solution.py:132
  63.4 1.5 %collective-permute-start.6 = (bf16[256,1536]{1,0:T(8,128)(2,1)}, bf16[256,1536]{1,0:T(8,128)(2,1)}, u32[]{:S(2)}, u32[]{:S(2)}) collective-permute-start(bf16[256,1536]{1,0:T(8,128)(2,1)} %collective-permute-done.4.refs_4_.refs_7_), channel_id=1, source_target_pairs={{4,6},{6,4},{8,10},{10,8},{5,7},{7,5},{9,11},{11,9},{20,22},{22,20... | collective-permute-start | bytes 2359304 | tf_op jit(solution)/shard_map/ppermute | solution.py:132
  65.0 1.6 %collective-permute-start.2 = (bf16[512,896]{1,0:T(8,128)(2,1)S(1)}, bf16[512,896]{1,0:T(8,128)(2,1)}, u32[]{:S(2)}, u32[]{:S(2)}) collective-permute-start(bf16[512,896]{1,0:T(8,128)(2,1)S(1)} %collective-permute-done.1.refs_3_), channel_id=1, source_target_pairs={{4,6},{6,4},{8,10},{10,8},{5,7},{7,5},{9,11},{11,9},{20,22},{22,20... | collective-permute-start | bytes 2752520 | tf_op jit(solution)/shard_map/ppermute | solution.py:132
  66.8 1.5 %collective-permute-start.18 = (bf16[512,640]{1,0:T(8,128)(2,1)}, bf16[512,640]{1,0:T(8,128)(2,1)}, u32[]{:S(2)}, u32[]{:S(2)}) collective-permute-start(bf16[512,640]{1,0:T(8,128)(2,1)} %collective-permute-done.14.refs_7_), channel_id=1, source_target_pairs={{4,6},{6,4},{8,10},{10,8},{5,7},{7,5},{9,11},{11,9},{20,22},{22,20... | collective-permute-start | bytes 1966088 | tf_op jit(solution)/shard_map/ppermute | solution.py:132
  68.3 1.5 %collective-permute-start.16 = (bf16[512,640]{1,0:T(8,128)(2,1)}, bf16[512,640]{1,0:T(8,128)(2,1)}, u32[]{:S(2)}, u32[]{:S(2)}) collective-permute-start(bf16[512,640]{1,0:T(8,128)(2,1)} %collective-permute-done.15.refs_3_), channel_id=1, source_target_pairs={{4,6},{6,4},{8,10},{10,8},{5,7},{7,5},{9,11},{11,9},{20,22},{22,20... | collective-permute-start | bytes 1966088 | tf_op jit(solution)/shard_map/ppermute | solution.py:132
  69.9 1.1 copy-done.3
  71.4 24.4 %collective-permute-start.17 = (bf16[256,640]{1,0:T(8,128)(2,1)S(1)}, bf16[256,640]{1,0:T(8,128)(2,1)S(1)}, u32[]{:S(2)}, u32[]{:S(2)}) collective-permute-start(bf16[256,640]{1,0:T(8,128)(2,1)S(1)} %shard_map.75.refs_6_.refs_11_.refs_9_.refs_2_), channel_id=1, source_target_pairs={{0,4},{2,6},{12,8},{14,10},{1,5},{3,7},{13,9},{15,11},{16,20},{18,... | collective-permute-start | bytes 983048 | tf_op jit(solution)/shard_map/ppermute | solution.py:132
  95.9 1.0 copy-done.5
  96.9 2.9 %shard_map.80 = (f32[7,128,256]{2,1,0:T(8,128)S(1)}, f32[7,8,256]{2,1,0:T(8,128)S(1)}, bf16[512,640]{1,0:T(8,128)(2,1)S(1)}, bf16[512,640]{1,0:T(8,128)(2,1)S(1)...) custom-call(s32[2]{0:T(128)S(1)} %pad_add_fusion.3.refs_0_.info_ref, s32[216]{0:T(256)S(1)} %reshape.60.refs_1_, ...), custom_call_target="tpu_custom_call" | custom-call | flops 822083584 | bytes 3211264 | tf_op jit(solution)/shard_map/pallas_call | solution.py:402
  99.8 1.2 shard_map.81
  101.0 1.3 collective-permute-start.12
  102.3 1.4 %shard_map.77 = (f32[7,128,256]{2,1,0:T(8,128)S(1)}, f32[7,8,256]{2,1,0:T(8,128)S(1)}, f32[5,128,256]{2,1,0:T(8,128)S(1)}, f32[5,8,256]{2,1,0:T(8,128)S(1)}) custom-call(s32[2]{0:T(128)S(1)} %pad_add_fusion.3.refs_0_.info_ref, s32[216]{0:T(256)S(1)} %reshape.60.refs_1_, bf16[256,896]{1,0:T(8,128)(2,1)S(1)} %shard_map.73.refs_2_, ...), custom_call_target="tpu_custom_call" | custom-call | flops 603979776 | bytes 2359296 | tf_op jit(solution)/shard_map/pallas_call | solution.py:402
  103.7 2.4 %shard_map.78 = (f32[7,128,256]{2,1,0:T(8,128)S(1)}, f32[7,8,256]{2,1,0:T(8,128)S(1)}, f32[5,128,256]{2,1,0:T(8,128)S(1)}, f32[5,8,256]{2,1,0:T(8,128)S(1)}) custom-call(s32[2]{0:T(128)S(1)} %pad_add_fusion.3.refs_0_.info_ref, s32[216]{0:T(256)S(1)} %reshape.60.refs_1_, bf16[256,896]{1,0:T(8,128)(2,1)S(1)} %shard_map.73.refs_2_, ...), custom_call_target="tpu_custom_call" | custom-call | flops 637534208 | bytes 2490368 | tf_op jit(solution)/shard_map/pallas_call | solution.py:402
  106.1 1.3 collective-permute-start.13
  107.4 1.2 shard_map.79
  108.7 0.7 collective-permute-start.10
  109.3 1.5 %shard_map.83 = (f32[5,128,256]{2,1,0:T(8,128)S(1)}, f32[5,8,256]{2,1,0:T(8,128)S(1)}, f32[5,128,256]{2,1,0:T(8,128)S(1)}, f32[5,8,256]{2,1,0:T(8,128)S(1)}, bf16[256,640]{1,0:T(8,128)(2,1)S(1)}) custom-call(s32[2]{0:T(128)S(1)} %pad_add_fusion.3.refs_0_.info_ref, s32[216]{0:T(256)S(1)} %reshape.60.refs_1_, ...), custom_call_target="tpu_custom_call" | custom-call | flops 754974720 | bytes 2949120 | tf_op jit(solution)/shard_map/pallas_call | solution.py:402
  110.9 1.3 shard_map.85
  112.2 1.3 collective-permute-start.20
  113.5 1.3 collective-permute-start.21
  114.8 1.3 shard_map.84
  116.1 0.7 collective-permute-start.19
  116.8 4.7 %collective-permute-done.13.refs_3_ = bf16[128,896]{1,0:T(8,128)(2,1)S(1)} collective-permute-done((bf16[128,896]{1,0:T(8,128)(2,1)S(1)}, bf16[128,896]{1,0:T(8,128)(2,1)S(1)}, u32[]{:S(2)}, u32[]{:S(2)}) %collective-permute-start.13) | collective-permute-done | bytes 229408 | tf_op jit(solution)/shard_map/ppermute | solution.py:132
  121.5 1.3 shard_map.82.refs_0_
  122.8 10.4 %collective-permute-done.20.refs_3_ = bf16[128,640]{1,0:T(8,128)(2,1)S(1)} collective-permute-done((bf16[128,640]{1,0:T(8,128)(2,1)S(1)}, bf16[128,640]{1,0:T(8,128)(2,1)S(1)}, u32[]{:S(2)}, u32[]{:S(2)}) %collective-permute-start.20) | collective-permute-done | bytes 163872 | tf_op jit(solution)/shard_map/ppermute | solution.py:132
  133.2 2.5 %collective-permute-done.21.refs_4_ = bf16[128,640]{1,0:T(8,128)(2,1)S(1)} collective-permute-done((bf16[128,640]{1,0:T(8,128)(2,1)S(1)}, bf16[128,640]{1,0:T(8,128)(2,1)S(1)}, u32[]{:S(2)}, u32[]{:S(2)}) %collective-permute-start.21) | collective-permute-done | bytes 163872 | tf_op jit(solution)/shard_map/ppermute | solution.py:132
  135.7 1.3 shard_map.86
  (59 shorter events, 1.7 us)
Async XLA Ops:
  0.0 58.4 %collective-permute-start.3 = (bf16[256,1536]{1,0:T(8,128)(2,1)}, bf16[256,1536]{1,0:T(8,128)(2,1)}, u32[]{:S(2)}, u32[]{:S(2)}) collective-permute-start(bf16[256,1536]{1,0:T(8,128)(2,1)} %refs_0_.7), channel_id=1, source_target_pairs={{4,8},{6,10},{8,4},{10,6},{5,9},{7,11},{9,5},{11,7},{20,24},{22,26... | collective-permute-start | bytes 2359304 | tf_op jit(solution)/shard_map/ppermute | solution.py:132
  1.5 58.6 %collective-permute-start.4 = (bf16[256,1536]{1,0:T(8,128)(2,1)}, bf16[256,1536]{1,0:T(8,128)(2,1)}, u32[]{:S(2)}, u32[]{:S(2)}) collective-permute-start(bf16[256,1536]{1,0:T(8,128)(2,1)} %refs_1_.3), channel_id=1, source_target_pairs={{4,8},{6,10},{8,4},{10,6},{5,9},{7,11},{9,5},{11,7},{20,24},{22,26... | collective-permute-start | bytes 2359304 | tf_op jit(solution)/shard_map/ppermute | solution.py:132
  3.1 1.1 copy-start
  4.2 9.9 %copy-start.2 = (bf16[256,1536]{1,0:T(8,128)(2,1)S(1)}, bf16[256,1536]{1,0:T(8,128)(2,1)}, u32[]{:S(2)}) copy-start(bf16[256,1536]{1,0:T(8,128)(2,1)} %refs_0_.6) | copy-start | bytes 2359300
  5.3 10.2 %copy-start.1 = (bf16[256,1536]{1,0:T(8,128)(2,1)S(1)}, bf16[256,1536]{1,0:T(8,128)(2,1)}, u32[]{:S(2)}) copy-start(bf16[256,1536]{1,0:T(8,128)(2,1)} %refs_1_.3) | copy-start | bytes 2359300
  5.3 40.8 %collective-permute-start = (bf16[512,896]{1,0:T(8,128)(2,1)S(1)}, bf16[512,896]{1,0:T(8,128)(2,1)}, u32[]{:S(2)}, u32[]{:S(2)}) collective-permute-start(bf16[512,896]{1,0:T(8,128)(2,1)S(1)} %shard_map.74.refs_3_), channel_id=1, source_target_pairs={{0,4},{2,6},{12,8},{14,10},{1,5},{3,7},{13,9},{15,11},{16,20},{18,... | collective-permute-start | bytes 2752520 | tf_op jit(solution)/shard_map/ppermute | solution.py:132
  14.2 29.6 %collective-permute-start.11 = (bf16[256,896]{1,0:T(8,128)(2,1)S(1)}, bf16[256,896]{1,0:T(8,128)(2,1)S(1)}, u32[]{:S(2)}, u32[]{:S(2)}) collective-permute-start(bf16[256,896]{1,0:T(8,128)(2,1)S(1)} %shard_map.73.refs_2_), channel_id=1, source_target_pairs={{0,4},{2,6},{12,8},{14,10},{1,5},{3,7},{13,9},{15,11},{16,20},{18,... | collective-permute-start | bytes 1376264 | tf_op jit(solution)/shard_map/ppermute | solution.py:132
  16.5 2.3 %copy-start.6 = (s32[12,16,8]{1,2,0:T(8,128)S(1)}, s32[12,16,8]{1,2,0:T(8,128)}, u32[]{:S(2)}) copy-start(s32[12,16,8]{1,2,0:T(8,128)} %param.10) | copy-start | bytes 18436
  16.6 39.6 %collective-permute-start.14 = (bf16[512,640]{1,0:T(8,128)(2,1)S(1)}, bf16[512,640]{1,0:T(8,128)(2,1)}, u32[]{:S(2)}, u32[]{:S(2)}) collective-permute-start(bf16[512,640]{1,0:T(8,128)(2,1)S(1)} %shard_map.76.refs_7_.refs_3_), channel_id=1, source_target_pairs={{0,4},{2,6},{12,8},{14,10},{1,5},{3,7},{13,9},{15,11},{16,20},{18,... | collective-permute-start | bytes 1966088 | tf_op jit(solution)/shard_map/ppermute | solution.py:132
  18.9 0.7 copy-start.7
  43.8 0.8 copy-start.4
  44.6 17.2 %collective-permute-start.8 = (bf16[256,1536]{1,0:T(8,128)(2,1)}, bf16[256,1536]{1,0:T(8,128)(2,1)}, u32[]{:S(2)}, u32[]{:S(2)}) collective-permute-start(bf16[256,1536]{1,0:T(8,128)(2,1)} %refs_0_.7), channel_id=1, source_target_pairs={{4,6},{6,4},{8,10},{10,8},{5,7},{7,5},{9,11},{11,9},{20,22},{22,20... | collective-permute-start | bytes 2359304 | tf_op jit(solution)/shard_map/ppermute | solution.py:132
  46.1 18.8 %collective-permute-start.1 = (bf16[512,896]{1,0:T(8,128)(2,1)}, bf16[512,896]{1,0:T(8,128)(2,1)S(1)}, u32[]{:S(2)}, u32[]{:S(2)}) collective-permute-start(bf16[512,896]{1,0:T(8,128)(2,1)} %collective-permute-done.refs_7_.refs_10_), channel_id=1, source_target_pairs={{4,8},{6,10},{8,4},{10,6},{5,9},{7,11},{9,5},{11,7},{20,24},{22,26... | collective-permute-start | bytes 2752520 | tf_op jit(solution)/shard_map/ppermute | solution.py:132
  56.1 7.3 %collective-permute-start.9 = (bf16[256,1536]{1,0:T(8,128)(2,1)}, bf16[256,1536]{1,0:T(8,128)(2,1)}, u32[]{:S(2)}, u32[]{:S(2)}) collective-permute-start(bf16[256,1536]{1,0:T(8,128)(2,1)} %refs_1_.3), channel_id=1, source_target_pairs={{4,6},{6,4},{8,10},{10,8},{5,7},{7,5},{9,11},{11,9},{20,22},{22,20... | collective-permute-start | bytes 2359304 | tf_op jit(solution)/shard_map/ppermute | solution.py:132
  57.7 0.7 copy-start.8
  58.4 9.9 %collective-permute-start.5 = (bf16[256,1536]{1,0:T(8,128)(2,1)}, bf16[256,1536]{1,0:T(8,128)(2,1)}, u32[]{:S(2)}, u32[]{:S(2)}) collective-permute-start(bf16[256,1536]{1,0:T(8,128)(2,1)} %collective-permute-done.3.refs_3_.refs_6_), channel_id=1, source_target_pairs={{4,6},{6,4},{8,10},{10,8},{5,7},{7,5},{9,11},{11,9},{20,22},{22,20... | collective-permute-start | bytes 2359304 | tf_op jit(solution)/shard_map/ppermute | solution.py:132
  60.2 6.6 %collective-permute-start.15 = (bf16[512,640]{1,0:T(8,128)(2,1)}, bf16[512,640]{1,0:T(8,128)(2,1)}, u32[]{:S(2)}, u32[]{:S(2)}) collective-permute-start(bf16[512,640]{1,0:T(8,128)(2,1)} %collective-permute-done.14.refs_7_), channel_id=1, source_target_pairs={{4,8},{6,10},{8,4},{10,6},{5,9},{7,11},{9,5},{11,7},{20,24},{22,26... | collective-permute-start | bytes 1966088 | tf_op jit(solution)/shard_map/ppermute | solution.py:132
  61.7 34.1 %collective-permute-start.7 = (bf16[512,896]{1,0:T(8,128)(2,1)}, bf16[512,896]{1,0:T(8,128)(2,1)}, u32[]{:S(2)}, u32[]{:S(2)}) collective-permute-start(bf16[512,896]{1,0:T(8,128)(2,1)} %collective-permute-done.refs_7_.refs_10_), channel_id=1, source_target_pairs={{4,6},{6,4},{8,10},{10,8},{5,7},{7,5},{9,11},{11,9},{20,22},{22,20... | collective-permute-start | bytes 2752520 | tf_op jit(solution)/shard_map/ppermute | solution.py:132
  63.4 7.9 %collective-permute-start.6 = (bf16[256,1536]{1,0:T(8,128)(2,1)}, bf16[256,1536]{1,0:T(8,128)(2,1)}, u32[]{:S(2)}, u32[]{:S(2)}) collective-permute-start(bf16[256,1536]{1,0:T(8,128)(2,1)} %collective-permute-done.4.refs_4_.refs_7_), channel_id=1, source_target_pairs={{4,6},{6,4},{8,10},{10,8},{5,7},{7,5},{9,11},{11,9},{20,22},{22,20... | collective-permute-start | bytes 2359304 | tf_op jit(solution)/shard_map/ppermute | solution.py:132
  65.0 34.8 %collective-permute-start.2 = (bf16[512,896]{1,0:T(8,128)(2,1)S(1)}, bf16[512,896]{1,0:T(8,128)(2,1)}, u32[]{:S(2)}, u32[]{:S(2)}) collective-permute-start(bf16[512,896]{1,0:T(8,128)(2,1)S(1)} %collective-permute-done.1.refs_3_), channel_id=1, source_target_pairs={{4,6},{6,4},{8,10},{10,8},{5,7},{7,5},{9,11},{11,9},{20,22},{22,20... | collective-permute-start | bytes 2752520 | tf_op jit(solution)/shard_map/ppermute | solution.py:132
  66.8 42.5 %collective-permute-start.18 = (bf16[512,640]{1,0:T(8,128)(2,1)}, bf16[512,640]{1,0:T(8,128)(2,1)}, u32[]{:S(2)}, u32[]{:S(2)}) collective-permute-start(bf16[512,640]{1,0:T(8,128)(2,1)} %collective-permute-done.14.refs_7_), channel_id=1, source_target_pairs={{4,6},{6,4},{8,10},{10,8},{5,7},{7,5},{9,11},{11,9},{20,22},{22,20... | collective-permute-start | bytes 1966088 | tf_op jit(solution)/shard_map/ppermute | solution.py:132
  68.3 42.5 %collective-permute-start.16 = (bf16[512,640]{1,0:T(8,128)(2,1)}, bf16[512,640]{1,0:T(8,128)(2,1)}, u32[]{:S(2)}, u32[]{:S(2)}) collective-permute-start(bf16[512,640]{1,0:T(8,128)(2,1)} %collective-permute-done.15.refs_3_), channel_id=1, source_target_pairs={{4,6},{6,4},{8,10},{10,8},{5,7},{7,5},{9,11},{11,9},{20,22},{22,20... | collective-permute-start | bytes 1966088 | tf_op jit(solution)/shard_map/ppermute | solution.py:132
  69.9 1.1 copy-start.3
  71.4 37.3 %collective-permute-start.17 = (bf16[256,640]{1,0:T(8,128)(2,1)S(1)}, bf16[256,640]{1,0:T(8,128)(2,1)S(1)}, u32[]{:S(2)}, u32[]{:S(2)}) collective-permute-start(bf16[256,640]{1,0:T(8,128)(2,1)S(1)} %shard_map.75.refs_6_.refs_11_.refs_9_.refs_2_), channel_id=1, source_target_pairs={{0,4},{2,6},{12,8},{14,10},{1,5},{3,7},{13,9},{15,11},{16,20},{18,... | collective-permute-start | bytes 983048 | tf_op jit(solution)/shard_map/ppermute | solution.py:132
  95.9 1.0 copy-start.5
  101.0 15.1 %collective-permute-start.12 = (bf16[128,896]{1,0:T(8,128)(2,1)S(1)}, bf16[128,896]{1,0:T(8,128)(2,1)S(1)}, u32[]{:S(2)}, u32[]{:S(2)}) collective-permute-start(bf16[128,896]{1,0:T(8,128)(2,1)S(1)} %get-tuple-element.43), channel_id=1, source_target_pairs={{4,0},{5,1},{6,2},{7,3},{8,12},{9,13},{10,14},{11,15},{20,16},{21,... | collective-permute-start | bytes 688136 | tf_op jit(solution)/shard_map/ppermute | solution.py:132
  106.1 15.3 %collective-permute-start.13 = (bf16[128,896]{1,0:T(8,128)(2,1)S(1)}, bf16[128,896]{1,0:T(8,128)(2,1)S(1)}, u32[]{:S(2)}, u32[]{:S(2)}) collective-permute-start(bf16[128,896]{1,0:T(8,128)(2,1)S(1)} %get-tuple-element.44), channel_id=1, source_target_pairs={{4,1},{5,0},{6,3},{7,2},{8,13},{9,12},{10,15},{11,14},{20,17},{21,... | collective-permute-start | bytes 688136 | tf_op jit(solution)/shard_map/ppermute | solution.py:132
  108.7 12.8 %collective-permute-start.10 = (bf16[128,896]{1,0:T(8,128)(2,1)S(1)}, bf16[128,896]{1,0:T(8,128)(2,1)S(1)}, u32[]{:S(2)}, u32[]{:S(2)}) collective-permute-start(bf16[128,896]{1,0:T(8,128)(2,1)S(1)} %get-tuple-element.39), channel_id=1, source_target_pairs={{4,5},{5,4},{6,7},{7,6},{8,9},{9,8},{10,11},{11,10},{20,21},{21,20... | collective-permute-start | bytes 688136 | tf_op jit(solution)/shard_map/ppermute | solution.py:132
  112.2 21.0 %collective-permute-start.20 = (bf16[128,640]{1,0:T(8,128)(2,1)S(1)}, bf16[128,640]{1,0:T(8,128)(2,1)S(1)}, u32[]{:S(2)}, u32[]{:S(2)}) collective-permute-start(bf16[128,640]{1,0:T(8,128)(2,1)S(1)} %get-tuple-element.57), channel_id=1, source_target_pairs={{4,0},{5,1},{6,2},{7,3},{8,12},{9,13},{10,14},{11,15},{20,16},{21,... | collective-permute-start | bytes 491528 | tf_op jit(solution)/shard_map/ppermute | solution.py:132
  113.5 22.3 %collective-permute-start.21 = (bf16[128,640]{1,0:T(8,128)(2,1)S(1)}, bf16[128,640]{1,0:T(8,128)(2,1)S(1)}, u32[]{:S(2)}, u32[]{:S(2)}) collective-permute-start(bf16[128,640]{1,0:T(8,128)(2,1)S(1)} %get-tuple-element.58), channel_id=1, source_target_pairs={{4,1},{5,0},{6,3},{7,2},{8,13},{9,12},{10,15},{11,14},{20,17},{21,... | collective-permute-start | bytes 491528 | tf_op jit(solution)/shard_map/ppermute | solution.py:132
  116.1 19.6 %collective-permute-start.19 = (bf16[128,640]{1,0:T(8,128)(2,1)S(1)}, bf16[128,640]{1,0:T(8,128)(2,1)S(1)}, u32[]{:S(2)}, u32[]{:S(2)}) collective-permute-start(bf16[128,640]{1,0:T(8,128)(2,1)S(1)} %get-tuple-element.53), channel_id=1, source_target_pairs={{4,5},{5,4},{6,7},{7,6},{8,9},{9,8},{10,11},{11,10},{20,21},{21,20... | collective-permute-start | bytes 491528 | tf_op jit(solution)/shard_map/ppermute | solution.py:132
